TPU v7x, 32 devices: a whole 2x2x4 slice. The times are simulated.
32 devices in a mesh: rep: 2 (over y), shard: 16 (over z, x, core).
Axes of the slice: x: 2, y: 2, z: 4, core: 2. Of those that a mesh axis runs over, the one named last changes fastest.
Arguments:
- activations: bfloat16 [32768, 2048], P(('rep', 'shard')), may hold values from -6 to 6
- cotangents: bfloat16 [32768, 1024], P(('rep', 'shard')), may hold values from -768 to 768
- inner_params: float32 [2, 2048, 1024], P('rep', 'shard'), may hold values from -6 to 6
- inner_moment: float32 [2, 2048, 1024], P('rep', 'shard'), may hold values from 0.25 to 4
- outer_params: float32 [2048, 1024], P('shard'), may hold values from -6 to 6
- momentum: float32 [2048, 1024], P('shard'), may hold values from -3 to 3
Outputs:
- new_params: float32 [2048, 1024], P('shard')
- new_momentum: float32 [2048, 1024], P('shard')
- compute_copy: bfloat16 [2048, 1024], replicated
All inputs are finite; a program needn't handle non-finite values.
Results may differ from a plain program's by a relative error of at most 0.007.
Values may be sent and summed in bfloat16 or wider, within the bound.
No kernel may reach another device: no remote copies, remote signals or barrier semaphores. Data moves between devices by JAX's collectives and lax.ppermute only.
A program may use at most 64 MiB of HBM per device.

v0:
```python
import jax
import jax.numpy as jnp
from jax import lax
from jax.sharding import PartitionSpec as P

outer_rate = 0.7
inertia = 0.9
inner_rate = 0.3
epsilon = 1e-08


def outer_step(pseudo_grad, outer_rows, moment_rows):
    fresh_moment = inertia * moment_rows + pseudo_grad
    fresh_params = outer_rows - outer_rate * (pseudo_grad + inertia * fresh_moment)
    return (fresh_params, fresh_moment)


def per_device(activations, cotangents, inner_params, inner_moment, outer_params, momentum):
    shard_count = lax.axis_size("shard")
    group_count = lax.axis_size("rep")
    group_tok = activations.shape[0] * shard_count
    summed = lax.psum_scatter(
        lax.dot_general(
            activations, cotangents, (((0,), (0,)), ((), ())), preferred_element_type=jnp.float32
        ).astype(jnp.bfloat16),
        "shard",
        scatter_dimension=0,
        tiled=True,
    ).astype(jnp.float32)
    mean_grad = summed / group_tok
    replica_params = inner_params[0] - inner_rate * mean_grad / (
        jnp.sqrt(inner_moment[0]) + epsilon
    )
    param_delta = outer_params - replica_params
    pseudo_grad = lax.psum(param_delta, "rep") / group_count
    new_params, new_momentum = outer_step(pseudo_grad, outer_params, momentum)
    compute_copy = lax.all_gather(new_params.astype(jnp.bfloat16), "shard", axis=0, tiled=True)
    return (new_params, new_momentum, compute_copy)


def solution(mesh):
    in_specs = (
        P(("rep", "shard"), None),
        P(("rep", "shard"), None),
        P("rep", "shard", None),
        P("rep", "shard", None),
        P("shard", None),
        P("shard", None),
    )
    out_specs = (P("shard", None), P("shard", None), P())
    return jax.shard_map(
        per_device, mesh=mesh, in_specs=in_specs, out_specs=out_specs, check_vma=False
    )
```

profile of v0, /device:TPU:0, one launch (start us, length us, event | category | flops | bytes accessed | tf_op | source)
XLA Modules:
  0.0 187.6 jit_solution(9160050818108355666)
XLA Ops:
  7.2 0.0 copy-start
  7.2 0.0 reduce-scatter.2.cloned.1.call-start
  7.2 1.5 copy-done
  8.8 8.3 %convolution_convert_fusion = bf16[2048,1024]{1,0:T(8,128)(2,1)} fusion(bf16[1024,2048]{1,0:T(8,128)(2,1)} %param.6, bf16[1024,1024]{1,0:T(8,128)(2,1)S(1)} %copy-done), kind=kOutput, calls=%fused_computation | convolution fusion | flops 4297064448 | bytes 10485760 | tf_op jit(solution)/shard_map/dot_general | solution.py:23
  17.1 0.0 copy-start.1
  17.1 0.0 copy-start.2
  17.1 0.0 reduce-scatter.2.cloned.1.call-update
  17.1 0.0 all-reduce.2.cloned.1.call-start
  17.1 75.8 %reduce-scatter.2.cloned.1.call-done = bf16[128,1024]{1,0:T(8,128)(2,1)} async-done(((bf16[2048,1024]{1,0:T(8,128)(2,1)}), bf16[128,1024]{1,0:T(8,128)(2,1)}) %reduce-scatter.2.cloned.1.call-update) | async-done | bytes 262160 | tf_op jit(solution)/shard_map/reduce_scatter | solution.py:22
  92.9 0.0 copy-done.1
  92.9 0.0 copy-done.2
  92.9 2.1 %fusion.1 = f32[128,1024]{1,0:T(8,128)} fusion(f32[128,1024]{1,0:T(8,128)S(1)} %copy-done.1, f32[1,128,1024]{2,1,0:T(8,128)S(1)} %copy-done.2, f32[1,128,1024]{2,1,0:T(8,128)} %param.9, bf16[128,1024]{1,0:T(8,128)(2,1)} %reduce-scatter.2.cloned.1.call-done), kind=kLoop, calls=%fused_computation.3 | loop fusion | flops 786432 | bytes 2359296 | tf_op jit(solution)/shard_map/sub | solution.py:34
  95.0 0.0 all-reduce.2.cloned.1.call-update
  95.1 0.0 all-gather.2.cloned.1.call-start
  95.1 28.2 %all-reduce.2.cloned.1.call-done = f32[128,1024]{1,0:T(8,128)} async-done(((f32[128,1024]{1,0:T(8,128)}), f32[128,1024]{1,0:T(8,128)}) %all-reduce.2.cloned.1.call-update) | async-done | bytes 524304 | tf_op jit(solution)/shard_map/psum | solution.py:35
  123.3 2.5 %fusion.2 = (bf16[128,1024]{1,0:T(8,128)(2,1)}, f32[128,1024]{1,0:T(8,128)}, f32[128,1024]{1,0:T(8,128)}) fusion(f32[128,1024]{1,0:T(8,128)S(1)} %copy-done.1, f32[128,1024]{1,0:T(8,128)} %all-reduce.2.cloned.1.call-done, f32[128,1024]{1,0:T(8,128)} %param.11), kind=kLoop, calls=%fused_computation.6 | loop fusion | flops 1048576 | bytes 2883584 | tf_op jit(solution)/shard_map/convert_element_type | solution.py:37
  125.8 0.0 all-gather.2.cloned.1.call-update
  125.8 50.6 %all-gather.2.cloned.1.call-done = bf16[2048,1024]{1,0:T(8,128)(2,1)} async-done(((bf16[128,1024]{1,0:T(8,128)(2,1)}), bf16[2048,1024]{1,0:T(8,128)(2,1)}) %all-gather.2.cloned.1.call-update) | async-done | bytes 4194320 | tf_op jit(solution)/shard_map/all_gather | solution.py:37
  176.5 4.6 %copy.11 = bf16[2048,1024]{1,0:T(8,128)(2,1)} copy(bf16[2048,1024]{1,0:T(8,128)(2,1)} %all-gather.2.cloned.1.call-done) | data formatting | bytes 8388608
Async XLA Ops:
  7.2 1.6 copy-start
  7.2 85.7 %reduce-scatter.2.cloned.1.call-start = ((), (), s32[]{:S(2)}) async-start(), calls=%async_computation.1 | async-start | bytes 4456448 | tf_op jit(solution)/shard_map/reduce_scatter | solution.py:22
  17.1 75.8 %copy-start.1 = (f32[128,1024]{1,0:T(8,128)S(1)}, f32[128,1024]{1,0:T(8,128)}, u32[]{:S(2)}) copy-start(f32[128,1024]{1,0:T(8,128)} %param.10) | copy-start | bytes 1572868
  17.1 75.8 %copy-start.2 = (f32[1,128,1024]{2,1,0:T(8,128)S(1)}, f32[1,128,1024]{2,1,0:T(8,128)}, u32[]{:S(2)}) copy-start(f32[1,128,1024]{2,1,0:T(8,128)} %param.8) | copy-start | bytes 1572868
  17.1 106.2 %all-reduce.2.cloned.1.call-start = ((), (), s32[]{:S(2)}) async-start(), calls=%async_computation.2 | async-start | bytes 1048576 | tf_op jit(solution)/shard_map/psum | solution.py:35
  95.1 81.4 %all-gather.2.cloned.1.call-start = ((), (), s32[]{:S(2)}) async-start(), calls=%async_computation.3 | async-start | bytes 4456448 | tf_op jit(solution)/shard_map/all_gather | solution.py:37
Sparse Core Ops, SparseCore 0:
  17.2 75.6 reduce-scatter.1
  95.7 27.5 all-reduce.1
  126.1 50.3 all-gather.1
where the time goes:
time: 188 us
  waiting for transfers between devices  155 us (82%)
  between operations  13.8 us (7%)
  matrix products  8.29 us (4%)
  local copies, waits for them, and re-layouts  6.19 us (3%)
  other arithmetic  4.62 us (2%)
    reduce_scatter x1, waiting for transfers between devices, per_device(): lax.psum_scatter(lax.dot_general(activations, cotangents, (((0,), (0,)),...  75.8 us
    all_gather x1, waiting for transfers between devices, per_device(): lax.all_gather(new_params.astype(jnp.bfloat16), 'shard', axis=0, tiled=True)  50.6 us
    psum x1, waiting for transfers between devices, per_device(): pseudo_grad = lax.psum(param_delta, 'rep') / group_count  28.2 us
    dot_general x1, matrix products, per_device(): lax.dot_general(activations, cotangents, (((0,), (0,)), ((), ())), prefer...  8.29 us
    unnamed x7, local copies, waits for them, and re-layouts  6.19 us
  transfers between devices with their start and end apart: 3, of which 3 were waited for; matrix products, arithmetic and copies ran while one was open for 0% of the time, Pallas kernels for 0%

commit v1 on v0

--- a/solution.py
+++ b/solution.py
@@ -32,7 +32,7 @@
         jnp.sqrt(inner_moment[0]) + epsilon
     )
     param_delta = outer_params - replica_params
-    pseudo_grad = lax.psum(param_delta, "rep") / group_count
+    pseudo_grad = jnp.sum(lax.all_gather(param_delta, "rep"), axis=0) / group_count
     new_params, new_momentum = outer_step(pseudo_grad, outer_params, momentum)
     compute_copy = lax.all_gather(new_params.astype(jnp.bfloat16), "shard", axis=0, tiled=True)
     return (new_params, new_momentum, compute_copy)

time: 188 us -> 181 us (0.963)
  waiting for transfers between devices: 155 us -> 147 us
    psum x1 -> x0, waiting for transfers between devices: 28.2 us -> none  [per_device(): pseudo_grad = lax.psum(param_delta, 'rep') / group_count]
    all_gather x0 -> x1, waiting for transfers between devices: none -> 20.3 us  [per_device(): lax.all_gather(param_delta, 'rep')]
where the time goes in v1:
time: 181 us
  waiting for transfers between devices  147 us (81%)
  between operations  13.8 us (8%)
  matrix products  8.29 us (5%)
  local copies, waits for them, and re-layouts  6.19 us (3%)
  other arithmetic  5.78 us (3%)
    reduce_scatter x1, waiting for transfers between devices, per_device(): lax.psum_scatter(lax.dot_general(activations, cotangents, (((0,), (0,)),...  75.8 us
    all_gather x1, waiting for transfers between devices, per_device(): lax.all_gather(new_params.astype(jnp.bfloat16), 'shard', axis=0, tiled=True)  50.5 us
    all_gather x1, waiting for transfers between devices, per_device(): lax.all_gather(param_delta, 'rep')  20.3 us
    dot_general x1, matrix products, per_device(): lax.dot_general(activations, cotangents, (((0,), (0,)), ((), ())), prefer...  8.29 us
    unnamed x7, local copies, waits for them, and re-layouts  6.19 us
  transfers between devices with their start and end apart: 3, of which 3 were waited for; matrix products, arithmetic and copies ran while one was open for 0% of the time, Pallas kernels for 0%

profile of v1, /device:TPU:0, one launch (start us, length us, event | category | flops | bytes accessed | tf_op | source)
XLA Modules:
  0.0 180.8 jit_solution(5261960814553591373)
XLA Ops:
  7.2 0.0 copy-start
  7.2 0.0 reduce-scatter.2.cloned.1.call-start
  7.2 1.5 copy-done
  8.8 8.3 %convolution_convert_fusion = bf16[2048,1024]{1,0:T(8,128)(2,1)} fusion(bf16[1024,2048]{1,0:T(8,128)(2,1)} %param.6, bf16[1024,1024]{1,0:T(8,128)(2,1)S(1)} %copy-done), kind=kOutput, calls=%fused_computation | convolution fusion | flops 4297064448 | bytes 10485760 | tf_op jit(solution)/shard_map/dot_general | solution.py:23
  17.1 0.0 copy-start.1
  17.1 0.0 copy-start.2
  17.1 0.0 reduce-scatter.2.cloned.1.call-update
  17.1 0.0 all-gather.6.cloned.1.call-start
  17.1 75.8 %reduce-scatter.2.cloned.1.call-done = bf16[128,1024]{1,0:T(8,128)(2,1)} async-done(((bf16[2048,1024]{1,0:T(8,128)(2,1)}), bf16[128,1024]{1,0:T(8,128)(2,1)}) %reduce-scatter.2.cloned.1.call-update) | async-done | bytes 262160 | tf_op jit(solution)/shard_map/reduce_scatter | solution.py:22
  92.9 0.0 copy-done.1
  92.9 0.0 copy-done.2
  92.9 2.1 %fusion.1 = f32[128,1024]{1,0:T(8,128)} fusion(f32[128,1024]{1,0:T(8,128)S(1)} %copy-done.1, f32[1,128,1024]{2,1,0:T(8,128)S(1)} %copy-done.2, f32[1,128,1024]{2,1,0:T(8,128)} %param.9, bf16[128,1024]{1,0:T(8,128)(2,1)} %reduce-scatter.2.cloned.1.call-done), kind=kLoop, calls=%fused_computation.3 | loop fusion | flops 786432 | bytes 2359296 | tf_op jit(solution)/shard_map/sub | solution.py:34
  95.0 0.0 all-gather.6.cloned.1.call-update
  95.1 0.0 all-gather.4.cloned.1.call-start
  95.1 20.3 %all-gather.6.cloned.1.call-done = f32[256,1024]{1,0:T(8,128)} async-done(((f32[128,1024]{1,0:T(8,128)}), f32[256,1024]{1,0:T(8,128)}) %all-gather.6.cloned.1.call-update) | async-done | bytes 1048592 | tf_op jit(solution)/shard_map/all_gather | solution.py:35
  115.4 1.3 reduce_sum.9
  116.7 2.3 %fusion.2 = (bf16[128,1024]{1,0:T(8,128)(2,1)}, f32[128,1024]{1,0:T(8,128)}, f32[128,1024]{1,0:T(8,128)}) fusion(f32[128,1024]{1,0:T(8,128)S(1)} %copy-done.1, f32[128,1024]{1,0:T(8,128)S(1)} %reduce_sum.9, f32[128,1024]{1,0:T(8,128)} %param.11), kind=kLoop, calls=%fused_computation.6 | loop fusion | flops 1048576 | bytes 2883584 | tf_op jit(solution)/shard_map/convert_element_type | solution.py:37
  119.0 0.0 all-gather.4.cloned.1.call-update
  119.1 50.5 %all-gather.4.cloned.1.call-done = bf16[2048,1024]{1,0:T(8,128)(2,1)} async-done(((bf16[128,1024]{1,0:T(8,128)(2,1)}), bf16[2048,1024]{1,0:T(8,128)(2,1)}) %all-gather.4.cloned.1.call-update) | async-done | bytes 4194320 | tf_op jit(solution)/shard_map/all_gather | solution.py:37
  169.6 4.6 %copy.10 = bf16[2048,1024]{1,0:T(8,128)(2,1)} copy(bf16[2048,1024]{1,0:T(8,128)(2,1)} %all-gather.4.cloned.1.call-done) | data formatting | bytes 8388608
Async XLA Ops:
  7.2 1.6 copy-start
  7.2 85.7 %reduce-scatter.2.cloned.1.call-start = ((), (), s32[]{:S(2)}) async-start(), calls=%async_computation.1 | async-start | bytes 4456448 | tf_op jit(solution)/shard_map/reduce_scatter | solution.py:22
  17.1 75.8 %copy-start.1 = (f32[128,1024]{1,0:T(8,128)S(1)}, f32[128,1024]{1,0:T(8,128)}, u32[]{:S(2)}) copy-start(f32[128,1024]{1,0:T(8,128)} %param.10) | copy-start | bytes 1572868
  17.1 75.8 %copy-start.2 = (f32[1,128,1024]{2,1,0:T(8,128)S(1)}, f32[1,128,1024]{2,1,0:T(8,128)}, u32[]{:S(2)}) copy-start(f32[1,128,1024]{2,1,0:T(8,128)} %param.8) | copy-start | bytes 1572868
  17.1 98.3 %all-gather.6.cloned.1.call-start = ((), (), s32[]{:S(2)}) async-start(), calls=%async_computation.3 | async-start | bytes 1572864 | tf_op jit(solution)/shard_map/all_gather | solution.py:35
  95.1 74.5 %all-gather.4.cloned.1.call-start = ((), (), s32[]{:S(2)}) async-start(), calls=%async_computation.2 | async-start | bytes 4456448 | tf_op jit(solution)/shard_map/all_gather | solution.py:37
Sparse Core Ops, SparseCore 0:
  17.2 75.6 reduce-scatter.1
  95.2 20.1 all-gather.5
  119.2 50.3 all-gather.3
